TPU v7x, 32 devices: a whole 2x2x4 slice. The times are simulated.
32 devices in a mesh: brick: 16 (over z, y, core), chan: 2 (over x).
Axes of the slice: x: 2, y: 2, z: 4, core: 2. Of those that a mesh axis runs over, the one named last changes fastest.
Arguments:
- volume: bfloat16 [32, 16, 64, 256], P('brick', 'chan'), may hold values from -6 to 6
- first_weight: bfloat16 [3, 3, 3, 256, 256], replicated, may hold values from -0.078125 to 0.078125
- second_weight: bfloat16 [3, 3, 3, 256, 256], replicated, may hold values from -0.078125 to 0.078125
- coarse_weight: bfloat16 [3, 3, 3, 256, 512], P(None, None, None, None, 'chan'), may hold values from -0.078125 to 0.078125
- projection: bfloat16 [512, 256], P('chan'), may hold values from -0.25 to 0.25
Outputs:
- merged: bfloat16 [32, 16, 64, 256], P('brick', 'chan')
All inputs are finite; a program needn't handle non-finite values.
Results may differ from a plain program's by a relative error of at most 0.011.
Values may be sent and summed in bfloat16 or wider, within the bound.
No kernel may reach another device: no remote copies, remote signals or barrier semaphores. Data moves between devices by JAX's collectives and lax.ppermute only.
A program may use at most 64 MiB of HBM per device.

v0:
```python
import functools

import jax
import jax.numpy as jnp
from jax import lax
from jax.experimental import pallas as pl
from jax.experimental.pallas import tpu as pltpu
from jax.sharding import PartitionSpec as P


AXES = ("brick", "chan")
BF16 = jnp.bfloat16
F32 = jnp.float32
LANES = 128
WEIGHT_COPY_FLOPS = 2**33
VMEM_SPEC = pl.BlockSpec(memory_space=pltpu.VMEM)


def brick_partner(kind, brick, bricks):
    if kind == "own":
        return brick
    partner = brick ^ 1 if kind == "near" else ((brick + 1) ^ 1) - 1
    return partner if 0 <= partner < bricks else None


def exchange(value, kind, chan_of):
    bricks, chans = lax.axis_size("brick"), lax.axis_size("chan")
    pairs = []
    for brick in range(bricks):
        for chan in range(chans):
            other, target = brick_partner(kind, brick, bricks), chan_of(chan)
            if other is not None and target is not None and 0 <= target < chans:
                pairs.append((brick * chans + chan, other * chans + target))
    return lax.ppermute(value, AXES, pairs)


def send_edges(volume_ref, *edges, chans):
    chan = lax.axis_index("chan")
    size_y = volume_ref.shape[1]
    for index, edge in enumerate(edges):
        start = jnp.where(chan == 0, size_y - 2, 0) if chans == 2 else (size_y - 2) * (1 - index)
        edge[...] = volume_ref[:, pl.ds(start, 2)]


def call(kernel, inputs, outputs, scratch, flops, limit_mib, results_in_vmem=True):
    inputs = [pltpu.with_memory_space_constraint(value, pltpu.VMEM) for value in inputs]
    if results_in_vmem:
        out_shape = [pltpu.VMEM(shape, dtype) for shape, dtype in outputs]
    else:
        out_shape = [jax.ShapeDtypeStruct(shape, dtype) for shape, dtype in outputs]
    return pl.pallas_call(
        kernel,
        out_shape=out_shape,
        in_specs=[VMEM_SPEC] * len(inputs),
        out_specs=[VMEM_SPEC] * len(outputs),
        scratch_shapes=scratch,
        compiler_params=pltpu.CompilerParams(vmem_limit_bytes=limit_mib * 2**20),
        cost_estimate=pl.CostEstimate(flops=flops, bytes_accessed=2**20, transcendentals=0),
    )(*inputs)


def tile_of(rows):
    return max(lines for lines in range(1, 10) if rows % lines == 0)


def conv_lines(terms, row, lines, weight):
    sums = []
    for dz in range(3):
        total = None
        for ref, plane, dx in terms:
            for dy in range(3):
                window = ref[plane, pl.ds(row + dy, lines)]
                window = window.reshape(lines * window.shape[1], window.shape[2])
                part = jnp.dot(window, weight[dx, dy, dz], preferred_element_type=F32)
                total = part if total is None else total + part
        sums.append(total)
    depth = terms[0][0].shape[2]
    count = sums[0].shape[0]
    place = lax.rem(lax.broadcasted_iota(jnp.int32, sums[0].shape, 0), depth)
    before = jnp.where(place == 0, 0.0, pltpu.roll(sums[0], 1, 0))
    after = jnp.where(place == depth - 1, 0.0, pltpu.roll(sums[2], count - 1, 0))
    return (before + sums[1] + after).reshape(lines, depth, sums[0].shape[1])


def tap(step, odd):
    return step + odd * (2 - 2 * step)


def halo_plan(chans, size_y):
    chan = lax.axis_index("chan")
    if chans == 1:
        return []
    if chans == 2:
        return [(jnp.where(chan == 1, 0, size_y + 2), jnp.where(chan == 1, size_y + 2, 0))]
    return [(0, None), (size_y + 2, None)]


def fill_planes(target, slot, plane, block, halos, chans):
    size_y = block.shape[1]
    target[slot, 2 : size_y + 2] = block[plane]
    zeros = jnp.zeros((2,) + target.shape[2:], target.dtype)
    if chans == 1:
        target[slot, 0:2] = zeros
        target[slot, size_y + 2 : size_y + 4] = zeros
    for (place, empty), halo in zip(halo_plan(chans, size_y), halos):
        target[slot, pl.ds(place, 2)] = halo[plane]
        if empty is not None:
            target[slot, pl.ds(empty, 2)] = zeros


def first_row(chans):
    if chans == 1:
        return 0
    if chans == 2:
        return -lax.axis_index("chan")
    return -1


def clear_outside(layer, slot, chans):
    chan = lax.axis_index("chan")
    last = layer.shape[1] - 1
    for row, owner in ((0, 0), (last, chans - 1)):
        if chans <= 2:
            keep = jnp.logical_and(chans == 2, chan != owner)
        else:
            keep = chan != owner
        layer[slot, row] = jnp.where(keep, layer[slot, row], jnp.zeros_like(layer[slot, row]))


def kernel_a(*refs, chans, halo_count):
    own, own_halos = refs[0], refs[1 : 1 + halo_count]
    near, near_halos = refs[1 + halo_count], refs[2 + halo_count : 2 + 2 * halo_count]
    weight_one, weight_two, layer_far, layer_own, out_far, out_near, field, layer = refs[2 + 2 * halo_count :]
    odd = lax.rem(lax.axis_index("brick"), 2)
    size_y = own.shape[1]
    fill_planes(field, 0, odd, own, own_halos, chans)
    fill_planes(field, 1, 1 - odd, own, own_halos, chans)
    fill_planes(field, 2, odd, near, near_halos, chans)
    fill_planes(field, 3, 1 - odd, near, near_halos, chans)
    start = first_row(chans)
    rows = layer_far.shape[0]
    lines = tile_of(rows)
    for row in range(0, rows, lines):
        base = start + row + 1
        for slot in range(2):
            terms = [(field, slot + step, tap(step, odd)) for step in range(3)]
            value = jnp.maximum(conv_lines(terms, base, lines, weight_one), 0.0).astype(BF16)
            layer[slot, pl.ds(start + row + 1, lines)] = value
    for slot in range(2):
        clear_outside(layer, slot, chans)
    lines_out = tile_of(size_y)
    for row in range(0, size_y, lines_out):
        out_far[pl.ds(row, lines_out)] = conv_lines([(layer, 0, tap(2, odd))], row, lines_out, weight_two)
        out_near[pl.ds(row, lines_out)] = conv_lines(
            [(layer, 0, tap(1, odd)), (layer, 1, tap(2, odd))], row, lines_out, weight_two
        )
    for row in range(0, rows, lines):
        base = start + row + 1
        layer_own[pl.ds(row, lines)] = conv_lines(
            [(field, 0, tap(1, odd)), (field, 1, tap(2, odd))], base, lines, weight_one
        )
        layer_far[pl.ds(row, lines)] = conv_lines([(field, 0, tap(2, odd))], base, lines, weight_one)


def kernel_b(*refs, chans, halo_count):
    far, far_halos = refs[0], refs[1 : 1 + halo_count]
    layer_far, layer_own, out_far, out_near, weight_one, weight_two = refs[1 + halo_count : 7 + halo_count]
    skipped, pooled, field, layer, sums = refs[7 + halo_count :]
    brick = lax.axis_index("brick")
    odd = lax.rem(brick, 2)
    size_y, depth = far.shape[1], far.shape[2]
    fill_planes(field, 0, odd, far, far_halos, chans)
    fill_planes(field, 1, 1 - odd, far, far_halos, chans)
    inside = jnp.logical_and(brick + odd > 0, brick + odd < lax.axis_size("brick"))
    start = first_row(chans)
    rows = layer_far.shape[0]
    lines = tile_of(rows)
    for row in range(0, rows, lines):
        base = start + row + 1
        value = conv_lines([(field, 0, tap(0, odd)), (field, 1, tap(1, odd))], base, lines, weight_one)
        value = jnp.maximum(value + layer_far[pl.ds(row, lines)], 0.0)
        layer[0, pl.ds(base, lines)] = jnp.where(inside, value, 0.0).astype(BF16)
        value = conv_lines([(field, 1, tap(0, odd))], base, lines, weight_one)
        value = jnp.maximum(value + layer_own[pl.ds(row, lines)], 0.0)
        layer[1, pl.ds(base, lines)] = value.astype(BF16)
    for slot in range(2):
        clear_outside(layer, slot, chans)
    lines_out = tile_of(size_y)
    for row in range(0, size_y, lines_out):
        spot = pl.ds(row, lines_out)
        value = conv_lines([(layer, 0, tap(0, odd)), (layer, 1, tap(1, odd))], row, lines_out, weight_two)
        first = jnp.maximum(value + out_far[spot], 0.0).astype(BF16)
        skipped[odd, spot] = first
        value = conv_lines([(layer, 1, tap(0, odd))], row, lines_out, weight_two)
        second = jnp.maximum(value + out_near[spot], 0.0).astype(BF16)
        skipped[1 - odd, spot] = second
        both = first.astype(F32) + second.astype(F32)
        for group in range(sums.shape[0]):
            sums[group, spot] = both[:, :, group * LANES : (group + 1) * LANES]
    for row in range(size_y // 2):
        for group in range(sums.shape[0]):
            pairs = [
                sums[group, 2 * row + step, pl.ds(side, depth // 2, stride=2)] for step in range(2) for side in range(2)
            ]
            mean = (pairs[0] + pairs[1] + pairs[2] + pairs[3]) * 0.125
            pooled[row, :, group * LANES : (group + 1) * LANES] = mean.astype(BF16)


def kernel_c(*refs, chans):
    blocks = refs[: 3 * chans]
    weight, projection = refs[3 * chans : 3 * chans + 2]
    own_part, sent = refs[3 * chans + 2], refs[3 * chans + 3 : 4 * chans + 2]
    field, parts = refs[4 * chans + 2 :]
    odd = lax.rem(lax.axis_index("brick"), 2)
    chan = lax.axis_index("chan")
    rows, depth = blocks[0].shape[0], blocks[0].shape[1]
    total = chans * rows
    for plane in range(3):
        zeros = jnp.zeros(field.shape[2:], field.dtype)
        field[plane, 0] = zeros
        field[plane, total + 1] = zeros
        for step in range(chans):
            source = lax.rem(chan - step + chans, chans)
            field[plane, pl.ds(1 + source * rows, rows)] = blocks[plane * chans + step][...]
    lines = tile_of(total)
    for row in range(0, total, lines):
        value = conv_lines([(field, step, tap(step, odd)) for step in range(3)], row, lines, weight)
        value = jnp.maximum(value, 0.0).astype(BF16).reshape(lines * depth, weight.shape[4])
        part = jnp.dot(value, projection[...], preferred_element_type=F32)
        parts[pl.ds(row, lines)] = part.reshape(lines, depth, part.shape[1])
    own_part[...] = parts[pl.ds(chan * rows, rows)]
    for step in range(1, chans):
        target = lax.rem(chan + step, chans)
        sent[step - 1][...] = parts[pl.ds(target * rows, rows)].astype(BF16)


def kernel_d(*refs):
    skipped, own_part = refs[0], refs[1]
    received, merged, fine = refs[2:-2], refs[-2], refs[-1]
    rows, depth = own_part.shape[0], own_part.shape[1]
    lifted = own_part[...]
    for part in received:
        lifted = lifted + part[...].astype(F32)
    for group in range(fine.shape[0]):
        lanes = slice(group * LANES, (group + 1) * LANES)
        for row in range(rows):
            for side in range(2):
                fine[group, row, pl.ds(side, depth, stride=2)] = lifted[row, :, lanes]
        for row in range(rows):
            value = fine[group, row]
            for plane in range(2):
                for step in range(2):
                    line = 2 * row + step
                    merged[plane, line, :, lanes] = (skipped[plane, line, :, lanes].astype(F32) + value).astype(BF16)


def shards(volume, first_weight, second_weight, coarse_weight, projection):
    chans = lax.axis_size("chan")
    size_x, size_y, depth, channels = volume.shape
    assert size_x == 2 and lax.axis_size("brick") % 2 == 0

    turns_of_edges = [[], [lambda c: 1 - c]][chans - 1] if chans <= 2 else [lambda c: c + 1, lambda c: c - 1]
    edges = []
    if chans > 1:
        edges = call(
            functools.partial(send_edges, chans=chans),
            [volume],
            [((2, 2, depth, channels), BF16)] * len(turns_of_edges),
            [],
            WEIGHT_COPY_FLOPS,
            16,
        )
    far = exchange(volume, "far", lambda c: c)
    own_halos = [exchange(edge, "own", turn) for edge, turn in zip(edges, turns_of_edges)]
    far_halos = [exchange(edge, "far", turn) for edge, turn in zip(edges, turns_of_edges)]
    near = exchange(volume, "near", lambda c: c)
    near_halos = [exchange(halo, "near", lambda c: c) for halo in own_halos]

    rows = size_y + min(chans - 1, 2)
    flops_of_plane = 2 * size_y * depth * 9 * channels * channels
    static = dict(chans=chans, halo_count=len(edges))
    partials = call(
        functools.partial(kernel_a, **static),
        [volume, *own_halos, near, *near_halos, first_weight, second_weight],
        [((rows, depth, channels), F32)] * 2 + [((size_y, depth, channels), F32)] * 2,
        [pltpu.VMEM((4, size_y + 4, depth, channels), BF16), pltpu.VMEM((2, size_y + 2, depth, channels), BF16)],
        12 * flops_of_plane,
        16,
    )
    skipped, pooled = call(
        functools.partial(kernel_b, **static),
        [far, *far_halos, *partials, first_weight, second_weight],
        [(volume.shape, BF16), ((size_y // 2, depth // 2, channels), BF16)],
        [
            pltpu.VMEM((2, size_y + 4, depth, channels), BF16),
            pltpu.VMEM((2, size_y + 2, depth, channels), BF16),
            pltpu.VMEM((channels // LANES, size_y, depth, LANES), F32),
        ],
        6 * flops_of_plane,
        16,
    )

    turns = [(lambda c, step=step: (c + step) % chans) for step in range(chans)]
    own_blocks = [pooled] + [exchange(pooled, "own", turn) for turn in turns[1:]]
    far_blocks = [exchange(pooled, "far", turns[0])]
    far_blocks += [exchange(pooled, "far", turn) for turn in turns[1:]]
    near_blocks = [exchange(pooled, "near", turns[0])]
    near_blocks += [exchange(block, "near", turns[0]) for block in own_blocks[1:]]
    part_shape = (size_y // 2, depth // 2, channels)
    coarse_rows = chans * size_y // 2
    parts = call(
        functools.partial(kernel_c, chans=chans),
        [*far_blocks, *own_blocks, *near_blocks, coarse_weight, projection],
        [(part_shape, F32)] + [(part_shape, BF16)] * (chans - 1),
        [
            pltpu.VMEM((3, coarse_rows + 2, depth // 2, channels), BF16),
            pltpu.VMEM((coarse_rows, depth // 2, channels), F32),
        ],
        2 * coarse_rows * (depth // 2) * 27 * channels * coarse_weight.shape[4],
        16,
    )
    received = [exchange(part, "own", turn) for part, turn in zip(parts[1:], turns[1:])]
    return call(
        kernel_d,
        [skipped, parts[0], *received],
        [(volume.shape, BF16)],
        [pltpu.VMEM((channels // LANES, size_y // 2, depth, LANES), F32)],
        volume.size,
        16,
        results_in_vmem=False,
    )[0]


def solution(mesh):
    in_specs = (
        P("brick", "chan", None, None),
        P(),
        P(),
        P(None, None, None, None, "chan"),
        P("chan", None),
    )
    out_specs = P("brick", "chan", None, None)

    return jax.shard_map(shards, mesh=mesh, in_specs=in_specs, out_specs=out_specs, check_vma=False)
```

profile of v0, /device:TPU:1, one launch (start us, length us, event | category | flops | bytes accessed | tf_op | source)
XLA Modules:
  0.0 49.6 jit_solution(13094929453381535972)
XLA Ops:
  0.0 0.0 copy-start.2
  0.0 0.0 collective-permute-start.3
  0.0 1.2 %copy-done.4 = bf16[2,8,64,256]{3,2,1,0:T(8,128)(2,1)S(1)} copy-done((bf16[2,8,64,256]{3,2,1,0:T(8,128)(2,1)S(1)}, bf16[2,8,64,256]{3,2,1,0:T(8,128)(2,1)}, u32[]{:S(2)}) %copy-start.4) | copy-done | bytes 524312
  1.2 2.9 %collective-permute-start.2 = (bf16[2,2,64,256]{3,2,1,0:T(8,128)(2,1)S(1)}, bf16[2,2,64,256]{3,2,1,0:T(8,128)(2,1)S(1)}, u32[]{:S(2)}, u32[]{:S(2)}) collective-permute-start(bf16[2,2,64,256]{3,2,1,0:T(8,128)(2,1)S(1)} %shard_map.55), channel_id=1, source_target_pairs={{0,1},{1,0},{2,3},{3,2},{4,5},{5,4},{6,7},{7,6},{8,9},{9,8},{10,11... | collective-permute-start | bytes 393224 | tf_op jit(solution)/shard_map/ppermute | solution.py:34
  4.2 4.0 %collective-permute-done.2.refs_1_ = bf16[2,2,64,256]{3,2,1,0:T(8,128)(2,1)S(1)} collective-permute-done((bf16[2,2,64,256]{3,2,1,0:T(8,128)(2,1)S(1)}, bf16[2,2,64,256]{3,2,1,0:T(8,128)(2,1)S(1)}, u32[]{:S(2)}, u32[]{:S(2)}) %collective-permute-start.2) | collective-permute-done | bytes 131104 | tf_op jit(solution)/shard_map/ppermute | solution.py:34
  8.2 0.4 collective-permute-start.4
  8.6 4.2 %collective-permute-start.1 = (bf16[2,2,64,256]{3,2,1,0:T(8,128)(2,1)S(1)}, bf16[2,2,64,256]{3,2,1,0:T(8,128)(2,1)S(1)}, u32[]{:S(2)}, u32[]{:S(2)}) collective-permute-start(bf16[2,2,64,256]{3,2,1,0:T(8,128)(2,1)S(1)} %shard_map.55), channel_id=1, source_target_pairs={{2,5},{3,4},{4,3},{5,2},{6,9},{7,8},{8,7},{9,6},{10,13},{11,12},{1... | collective-permute-start | bytes 393224 | tf_op jit(solution)/shard_map/ppermute | solution.py:34
  12.8 2.5 %collective-permute-start = (bf16[2,8,64,256]{3,2,1,0:T(8,128)(2,1)S(1)}, bf16[2,8,64,256]{3,2,1,0:T(8,128)(2,1)S(1)}, u32[]{:S(2)}, u32[]{:S(2)}) collective-permute-start(bf16[2,8,64,256]{3,2,1,0:T(8,128)(2,1)S(1)} %copy-done.4), channel_id=1, source_target_pairs={{2,4},{3,5},{4,2},{5,3},{6,8},{7,9},{8,6},{9,7},{10,12},{11,13},{1... | collective-permute-start | bytes 1572872 | tf_op jit(solution)/shard_map/ppermute | solution.py:34
  15.4 0.0 collective-permute-done.4.refs_3_
  15.4 0.0 collective-permute-done.3.refs_2_
  15.4 0.0 copy-done.2
  15.4 0.0 copy-done.3
  15.4 8.3 %shard_map.56 = (f32[9,64,256]{2,1,0:T(8,128)S(1)}, f32[9,64,256]{2,1,0:T(8,128)S(1)}, f32[8,64,256]{2,1,0:T(8,128)S(1)}, f32[8,64,256]{2,1,0:T(8,128)S(1)}) custom-call(bf16[2,8,64,256]{3,2,1,0:T(8,128)(2,1)S(1)} %copy-done.4, bf16[2,2,64,256]{3,2,1,0:T(8,128)(2,1)S(1)} %collective-permute-done.2.refs_1_, ...), custom_call_target="tpu_custom_call" | custom-call | flops 7247757312 | bytes 1048576 | tf_op jit(solution)/shard_map/pallas_call | solution.py:51
  23.8 0.0 collective-permute-done.1.refs_1_
  23.8 3.7 %collective-permute-done.refs_0_ = bf16[2,8,64,256]{3,2,1,0:T(8,128)(2,1)S(1)} collective-permute-done((bf16[2,8,64,256]{3,2,1,0:T(8,128)(2,1)S(1)}, bf16[2,8,64,256]{3,2,1,0:T(8,128)(2,1)S(1)}, u32[]{:S(2)}, u32[]{:S(2)}) %collective-permute-start) | collective-permute-done | bytes 524320 | tf_op jit(solution)/shard_map/ppermute | solution.py:34
  27.5 4.4 %shard_map.57 = (bf16[2,8,64,256]{3,2,1,0:T(8,128)(2,1)S(1)}, bf16[4,32,256]{2,1,0:T(8,128)(2,1)S(1)}) custom-call(bf16[2,8,64,256]{3,2,1,0:T(8,128)(2,1)S(1)} %collective-permute-done.refs_0_, bf16[2,2,64,256]{3,2,1,0:T(8,128)(2,1)S(1)} %collective-permute-done.1.refs_1_, f32[9,64,256]{2,1,0:T(8,128)S(1)} %get-tuple-element.13.refs_2_, ...), custom_call_target="tpu_custom_call" | custom-call | flops 3623878656 | bytes 1048576 | tf_op jit(solution)/shard_map/pallas_call | solution.py:51
  31.9 1.1 %collective-permute-start.7 = (bf16[4,32,256]{2,1,0:T(8,128)(2,1)S(1)}, bf16[4,32,256]{2,1,0:T(8,128)(2,1)S(1)}, u32[]{:S(2)}, u32[]{:S(2)}) collective-permute-start(bf16[4,32,256]{2,1,0:T(8,128)(2,1)S(1)} %get-tuple-element.18.refs_2_), channel_id=1, source_target_pairs={{0,1},{1,0},{2,3},{3,2},{4,5},{5,4},{6,7},{7,6},{8,9},{9,8},{10,11... | collective-permute-start | bytes 196616 | tf_op jit(solution)/shard_map/ppermute | solution.py:34
  33.0 4.7 %collective-permute-start.5 = (bf16[4,32,256]{2,1,0:T(8,128)(2,1)S(1)}, bf16[4,32,256]{2,1,0:T(8,128)(2,1)S(1)}, u32[]{:S(2)}, u32[]{:S(2)}) collective-permute-start(bf16[4,32,256]{2,1,0:T(8,128)(2,1)S(1)} %get-tuple-element.18.refs_2_), channel_id=1, source_target_pairs={{2,4},{3,5},{4,2},{5,3},{6,8},{7,9},{8,6},{9,7},{10,12},{11,13},{1... | collective-permute-start | bytes 196616 | tf_op jit(solution)/shard_map/ppermute | solution.py:34
  37.7 2.1 %collective-permute-start.6 = (bf16[4,32,256]{2,1,0:T(8,128)(2,1)S(1)}, bf16[4,32,256]{2,1,0:T(8,128)(2,1)S(1)}, u32[]{:S(2)}, u32[]{:S(2)}) collective-permute-start(bf16[4,32,256]{2,1,0:T(8,128)(2,1)S(1)} %get-tuple-element.18.refs_2_), channel_id=1, source_target_pairs={{2,5},{3,4},{4,3},{5,2},{6,9},{7,8},{8,7},{9,6},{10,13},{11,12},{1... | collective-permute-start | bytes 196616 | tf_op jit(solution)/shard_map/ppermute | solution.py:34
  39.8 0.1 collective-permute-start.8
  39.8 0.0 collective-permute-done.7.refs_3_
  39.9 0.5 collective-permute-start.9
  40.3 0.0 collective-permute-done.5.refs_0_
  40.3 3.8 %collective-permute-done.6.refs_1_ = bf16[4,32,256]{2,1,0:T(8,128)(2,1)S(1)} collective-permute-done((bf16[4,32,256]{2,1,0:T(8,128)(2,1)S(1)}, bf16[4,32,256]{2,1,0:T(8,128)(2,1)S(1)}, u32[]{:S(2)}, u32[]{:S(2)}) %collective-permute-start.6) | collective-permute-done | bytes 65568 | tf_op jit(solution)/shard_map/ppermute | solution.py:34
  44.2 0.0 collective-permute-done.8.refs_4_
  44.2 0.0 collective-permute-done.9.refs_5_
  44.2 0.0 copy-done
  44.2 0.0 copy-done.1
  44.2 1.3 %shard_map.58 = (f32[4,32,256]{2,1,0:T(8,128)S(1)}, bf16[4,32,256]{2,1,0:T(8,128)(2,1)S(1)}) custom-call(bf16[4,32,256]{2,1,0:T(8,128)(2,1)S(1)} %collective-permute-done.5.refs_0_, bf16[4,32,256]{2,1,0:T(8,128)(2,1)S(1)} %collective-permute-done.6.refs_1_, bf16[4,32,256]{2,1,0:T(8,128)(2,1)S(1)} %get-tuple-element.18.refs_2_, ...), custom_call_target="tpu_custom_call" | custom-call | flops 905969664 | bytes 1048576 | tf_op jit(solution)/shard_map/pallas_call | solution.py:51
  45.5 0.5 %collective-permute-start.10 = (bf16[4,32,256]{2,1,0:T(8,128)(2,1)S(1)}, bf16[4,32,256]{2,1,0:T(8,128)(2,1)S(1)}, u32[]{:S(2)}, u32[]{:S(2)}) collective-permute-start(bf16[4,32,256]{2,1,0:T(8,128)(2,1)S(1)} %get-tuple-element.20), channel_id=1, source_target_pairs={{0,1},{1,0},{2,3},{3,2},{4,5},{5,4},{6,7},{7,6},{8,9},{9,8},{10,11... | collective-permute-start | bytes 196616 | tf_op jit(solution)/shard_map/ppermute | solution.py:34
  46.0 2.7 %collective-permute-done.10.refs_2_ = bf16[4,32,256]{2,1,0:T(8,128)(2,1)S(1)} collective-permute-done((bf16[4,32,256]{2,1,0:T(8,128)(2,1)S(1)}, bf16[4,32,256]{2,1,0:T(8,128)(2,1)S(1)}, u32[]{:S(2)}, u32[]{:S(2)}) %collective-permute-start.10) | collective-permute-done | bytes 65568 | tf_op jit(solution)/shard_map/ppermute | solution.py:34
  48.7 0.9 %shard_map.59 = bf16[2,8,64,256]{3,2,1,0:T(8,128)(2,1)} custom-call(bf16[2,8,64,256]{3,2,1,0:T(8,128)(2,1)S(1)} %get-tuple-element.17.refs_0_, f32[4,32,256]{2,1,0:T(8,128)S(1)} %get-tuple-element.19.refs_1_, bf16[4,32,256]{2,1,0:T(8,128)(2,1)S(1)} %collective-permute-done.10.refs_2_), custom_call_target="tpu_custom_call" | custom-call | flops 262144 | bytes 1048576 | tf_op jit(solution)/shard_map/pallas_call | solution.py:51
  (5 shorter events, 0.0 us)
Async XLA Ops:
  0.0 15.4 %copy-start.2 = (bf16[3,3,3,256,256]{4,3,2,1,0:T(8,128)(2,1)S(1)}, bf16[3,3,3,256,256]{4,3,2,1,0:T(8,128)(2,1)}, u32[]{:S(2)}) copy-start(bf16[3,3,3,256,256]{4,3,2,1,0:T(8,128)(2,1)} %refs_6_.2) | copy-start | bytes 10616836
  0.0 15.4 %copy-start.3 = (bf16[3,3,3,256,256]{4,3,2,1,0:T(8,128)(2,1)S(1)}, bf16[3,3,3,256,256]{4,3,2,1,0:T(8,128)(2,1)}, u32[]{:S(2)}) copy-start(bf16[3,3,3,256,256]{4,3,2,1,0:T(8,128)(2,1)} %refs_7_.2) | copy-start | bytes 10616836
  0.0 15.4 %collective-permute-start.3 = (bf16[2,8,64,256]{3,2,1,0:T(8,128)(2,1)}, bf16[2,8,64,256]{3,2,1,0:T(8,128)(2,1)S(1)}, u32[]{:S(2)}, u32[]{:S(2)}) collective-permute-start(bf16[2,8,64,256]{3,2,1,0:T(8,128)(2,1)} %refs_0_.1), channel_id=1, source_target_pairs={{0,2},{1,3},{2,0},{3,1},{4,6},{5,7},{6,4},{7,5},{8,10},{9,11},{10,... | collective-permute-start | bytes 1572872 | tf_op jit(solution)/shard_map/ppermute | solution.py:34
  0.0 1.2 %copy-start.4 = (bf16[2,8,64,256]{3,2,1,0:T(8,128)(2,1)S(1)}, bf16[2,8,64,256]{3,2,1,0:T(8,128)(2,1)}, u32[]{:S(2)}) copy-start(bf16[2,8,64,256]{3,2,1,0:T(8,128)(2,1)} %refs_0_.1) | copy-start | bytes 1572868
  1.2 7.0 %collective-permute-start.2 = (bf16[2,2,64,256]{3,2,1,0:T(8,128)(2,1)S(1)}, bf16[2,2,64,256]{3,2,1,0:T(8,128)(2,1)S(1)}, u32[]{:S(2)}, u32[]{:S(2)}) collective-permute-start(bf16[2,2,64,256]{3,2,1,0:T(8,128)(2,1)S(1)} %shard_map.55), channel_id=1, source_target_pairs={{0,1},{1,0},{2,3},{3,2},{4,5},{5,4},{6,7},{7,6},{8,9},{9,8},{10,11... | collective-permute-start | bytes 393224 | tf_op jit(solution)/shard_map/ppermute | solution.py:34
  8.2 7.2 %collective-permute-start.4 = (bf16[2,2,64,256]{3,2,1,0:T(8,128)(2,1)S(1)}, bf16[2,2,64,256]{3,2,1,0:T(8,128)(2,1)S(1)}, u32[]{:S(2)}, u32[]{:S(2)}) collective-permute-start(bf16[2,2,64,256]{3,2,1,0:T(8,128)(2,1)S(1)} %collective-permute-done.2.refs_1_), channel_id=1, source_target_pairs={{0,2},{1,3},{2,0},{3,1},{4,6},{5,7},{6,4},{7,5},{8,10},{9,11},{10,... | collective-permute-start | bytes 393224 | tf_op jit(solution)/shard_map/ppermute | solution.py:34
  8.6 15.1 %collective-permute-start.1 = (bf16[2,2,64,256]{3,2,1,0:T(8,128)(2,1)S(1)}, bf16[2,2,64,256]{3,2,1,0:T(8,128)(2,1)S(1)}, u32[]{:S(2)}, u32[]{:S(2)}) collective-permute-start(bf16[2,2,64,256]{3,2,1,0:T(8,128)(2,1)S(1)} %shard_map.55), channel_id=1, source_target_pairs={{2,5},{3,4},{4,3},{5,2},{6,9},{7,8},{8,7},{9,6},{10,13},{11,12},{1... | collective-permute-start | bytes 393224 | tf_op jit(solution)/shard_map/ppermute | solution.py:34
  12.8 14.7 %collective-permute-start = (bf16[2,8,64,256]{3,2,1,0:T(8,128)(2,1)S(1)}, bf16[2,8,64,256]{3,2,1,0:T(8,128)(2,1)S(1)}, u32[]{:S(2)}, u32[]{:S(2)}) collective-permute-start(bf16[2,8,64,256]{3,2,1,0:T(8,128)(2,1)S(1)} %copy-done.4), channel_id=1, source_target_pairs={{2,4},{3,5},{4,2},{5,3},{6,8},{7,9},{8,6},{9,7},{10,12},{11,13},{1... | collective-permute-start | bytes 1572872 | tf_op jit(solution)/shard_map/ppermute | solution.py:34
  27.5 16.7 %copy-start = (bf16[3,3,3,256,256]{4,3,2,1,0:T(8,128)(2,1)S(1)}, bf16[3,3,3,256,256]{4,3,2,1,0:T(8,128)(2,1)}, u32[]{:S(2)}) copy-start(bf16[3,3,3,256,256]{4,3,2,1,0:T(8,128)(2,1)} %refs_6_.3) | copy-start | bytes 10616836
  27.5 16.7 %copy-start.1 = (bf16[256,256]{1,0:T(8,128)(2,1)S(1)}, bf16[256,256]{1,0:T(8,128)(2,1)}, u32[]{:S(2)}) copy-start(bf16[256,256]{1,0:T(8,128)(2,1)} %refs_7_.3) | copy-start | bytes 393220
  31.9 7.9 %collective-permute-start.7 = (bf16[4,32,256]{2,1,0:T(8,128)(2,1)S(1)}, bf16[4,32,256]{2,1,0:T(8,128)(2,1)S(1)}, u32[]{:S(2)}, u32[]{:S(2)}) collective-permute-start(bf16[4,32,256]{2,1,0:T(8,128)(2,1)S(1)} %get-tuple-element.18.refs_2_), channel_id=1, source_target_pairs={{0,1},{1,0},{2,3},{3,2},{4,5},{5,4},{6,7},{7,6},{8,9},{9,8},{10,11... | collective-permute-start | bytes 196616 | tf_op jit(solution)/shard_map/ppermute | solution.py:34
  33.0 7.3 %collective-permute-start.5 = (bf16[4,32,256]{2,1,0:T(8,128)(2,1)S(1)}, bf16[4,32,256]{2,1,0:T(8,128)(2,1)S(1)}, u32[]{:S(2)}, u32[]{:S(2)}) collective-permute-start(bf16[4,32,256]{2,1,0:T(8,128)(2,1)S(1)} %get-tuple-element.18.refs_2_), channel_id=1, source_target_pairs={{2,4},{3,5},{4,2},{5,3},{6,8},{7,9},{8,6},{9,7},{10,12},{11,13},{1... | collective-permute-start | bytes 196616 | tf_op jit(solution)/shard_map/ppermute | solution.py:34
  37.7 6.5 %collective-permute-start.6 = (bf16[4,32,256]{2,1,0:T(8,128)(2,1)S(1)}, bf16[4,32,256]{2,1,0:T(8,128)(2,1)S(1)}, u32[]{:S(2)}, u32[]{:S(2)}) collective-permute-start(bf16[4,32,256]{2,1,0:T(8,128)(2,1)S(1)} %get-tuple-element.18.refs_2_), channel_id=1, source_target_pairs={{2,5},{3,4},{4,3},{5,2},{6,9},{7,8},{8,7},{9,6},{10,13},{11,12},{1... | collective-permute-start | bytes 196616 | tf_op jit(solution)/shard_map/ppermute | solution.py:34
  39.8 4.4 %collective-permute-start.8 = (bf16[4,32,256]{2,1,0:T(8,128)(2,1)S(1)}, bf16[4,32,256]{2,1,0:T(8,128)(2,1)S(1)}, u32[]{:S(2)}, u32[]{:S(2)}) collective-permute-start(bf16[4,32,256]{2,1,0:T(8,128)(2,1)S(1)} %get-tuple-element.18.refs_2_), channel_id=1, source_target_pairs={{0,2},{1,3},{2,0},{3,1},{4,6},{5,7},{6,4},{7,5},{8,10},{9,11},{10,... | collective-permute-start | bytes 196616 | tf_op jit(solution)/shard_map/ppermute | solution.py:34
  39.9 4.3 %collective-permute-start.9 = (bf16[4,32,256]{2,1,0:T(8,128)(2,1)S(1)}, bf16[4,32,256]{2,1,0:T(8,128)(2,1)S(1)}, u32[]{:S(2)}, u32[]{:S(2)}) collective-permute-start(bf16[4,32,256]{2,1,0:T(8,128)(2,1)S(1)} %collective-permute-done.7.refs_3_), channel_id=1, source_target_pairs={{0,2},{1,3},{2,0},{3,1},{4,6},{5,7},{6,4},{7,5},{8,10},{9,11},{10,... | collective-permute-start | bytes 196616 | tf_op jit(solution)/shard_map/ppermute | solution.py:34
  45.5 3.2 %collective-permute-start.10 = (bf16[4,32,256]{2,1,0:T(8,128)(2,1)S(1)}, bf16[4,32,256]{2,1,0:T(8,128)(2,1)S(1)}, u32[]{:S(2)}, u32[]{:S(2)}) collective-permute-start(bf16[4,32,256]{2,1,0:T(8,128)(2,1)S(1)} %get-tuple-element.20), channel_id=1, source_target_pairs={{0,1},{1,0},{2,3},{3,2},{4,5},{5,4},{6,7},{7,6},{8,9},{9,8},{10,11... | collective-permute-start | bytes 196616 | tf_op jit(solution)/shard_map/ppermute | solution.py:34
where the time goes:
time: 49.8 us; the launch traced here: 49.6 us
  starting transfers between devices  19 us (38%)
  Pallas kernels  15 us (30%)
  waiting for transfers between devices  14.3 us (29%)
  local copies, waits for them, and re-layouts  1.21 us (2%)
    ppermute x11, starting transfers between devices, exchange(): return lax.ppermute(value, AXES, pairs)  19 us
    pallas_call x5, Pallas kernels, call(): pl.pallas_call(kernel, out_shape=out_shape, in_specs=[VMEM_SPEC] * len(in...  15 us
    ppermute x11, waiting for transfers between devices, exchange(): return lax.ppermute(value, AXES, pairs)  14.3 us
    unnamed x10, local copies, waits for them, and re-layouts  1.21 us
  transfers between devices with their start and end apart: 11, of which 4 were waited for; matrix products, arithmetic and copies ran while one was open for 0% of the time, Pallas kernels for 17%

commit v1 on v0

--- a/solution.py
+++ b/solution.py
@@ -34,12 +34,23 @@
     return lax.ppermute(value, AXES, pairs)
 
 
-def send_edges(volume_ref, *edges, chans):
+def row_split(chans, size_y):
     chan = lax.axis_index("chan")
-    size_y = volume_ref.shape[1]
-    for index, edge in enumerate(edges):
-        start = jnp.where(chan == 0, size_y - 2, 0) if chans == 2 else (size_y - 2) * (1 - index)
-        edge[...] = volume_ref[:, pl.ds(start, 2)]
+    if chans == 1:
+        return [], (0, size_y)
+    if chans == 2:
+        return [(jnp.where(chan == 0, size_y - 2, 0), 2)], (jnp.where(chan == 0, 0, 2), size_y - 2)
+    return [(size_y - 2, 2), (0, 2)], (2, size_y - 4)
+
+
+def early(out):
+    out[...] = jnp.zeros_like(out)
+
+
+def split_rows(volume, _, *pieces, chans):
+    sides, rest = row_split(chans, volume.shape[1])
+    for piece, (start, count) in zip(pieces, [*sides, rest]):
+        piece[...] = volume[:, pl.ds(start, count)]
 
 
 def call(kernel, inputs, outputs, scratch, flops, limit_mib, results_in_vmem=True):
@@ -95,9 +106,10 @@
     return [(0, None), (size_y + 2, None)]
 
 
-def fill_planes(target, slot, plane, block, halos, chans):
-    size_y = block.shape[1]
-    target[slot, 2 : size_y + 2] = block[plane]
+def fill_planes(target, slot, plane, pieces, halos, chans):
+    size_y = target.shape[1] - 4
+    for start, block in pieces:
+        target[slot, pl.ds(start + 2, block.shape[1])] = block[plane]
     zeros = jnp.zeros((2,) + target.shape[2:], target.dtype)
     if chans == 1:
         target[slot, 0:2] = zeros
@@ -133,10 +145,10 @@
     weight_one, weight_two, layer_far, layer_own, out_far, out_near, field, layer = refs[2 + 2 * halo_count :]
     odd = lax.rem(lax.axis_index("brick"), 2)
     size_y = own.shape[1]
-    fill_planes(field, 0, odd, own, own_halos, chans)
-    fill_planes(field, 1, 1 - odd, own, own_halos, chans)
-    fill_planes(field, 2, odd, near, near_halos, chans)
-    fill_planes(field, 3, 1 - odd, near, near_halos, chans)
+    fill_planes(field, 0, odd, [(0, own)], own_halos, chans)
+    fill_planes(field, 1, 1 - odd, [(0, own)], own_halos, chans)
+    fill_planes(field, 2, odd, [(0, near)], near_halos, chans)
+    fill_planes(field, 3, 1 - odd, [(0, near)], near_halos, chans)
     start = first_row(chans)
     rows = layer_far.shape[0]
     lines = tile_of(rows)
@@ -163,12 +175,14 @@
 
 
 def kernel_b(*refs, chans, halo_count):
-    far, far_halos = refs[0], refs[1 : 1 + halo_count]
-    layer_far, layer_own, out_far, out_near, weight_one, weight_two = refs[1 + halo_count : 7 + halo_count]
-    skipped, pooled, field, layer, sums = refs[7 + halo_count :]
+    rest, edges, far_halos = refs[0], refs[1 : 1 + halo_count], refs[1 + halo_count : 1 + 2 * halo_count]
+    layer_far, layer_own, out_far, out_near, weight_one, weight_two = refs[1 + 2 * halo_count : 7 + 2 * halo_count]
+    skipped, pooled, field, layer, sums = refs[7 + 2 * halo_count :]
     brick = lax.axis_index("brick")
     odd = lax.rem(brick, 2)
-    size_y, depth = far.shape[1], far.shape[2]
+    size_y, depth = out_far.shape[0], out_far.shape[1]
+    sides, between = row_split(chans, size_y)
+    far = [(start, edge) for (start, _), edge in zip(sides, edges)] + [(between[0], rest)]
     fill_planes(field, 0, odd, far, far_halos, chans)
     fill_planes(field, 1, 1 - odd, far, far_halos, chans)
     inside = jnp.logical_and(brick + odd > 0, brick + odd < lax.axis_size("brick"))
@@ -259,26 +273,28 @@
     size_x, size_y, depth, channels = volume.shape
     assert size_x == 2 and lax.axis_size("brick") % 2 == 0
 
-    turns_of_edges = [[], [lambda c: 1 - c]][chans - 1] if chans <= 2 else [lambda c: c + 1, lambda c: c - 1]
-    edges = []
-    if chans > 1:
-        edges = call(
-            functools.partial(send_edges, chans=chans),
-            [volume],
-            [((2, 2, depth, channels), BF16)] * len(turns_of_edges),
-            [],
-            WEIGHT_COPY_FLOPS,
-            16,
-        )
-    far = exchange(volume, "far", lambda c: c)
-    own_halos = [exchange(edge, "own", turn) for edge, turn in zip(edges, turns_of_edges)]
-    far_halos = [exchange(edge, "far", turn) for edge, turn in zip(edges, turns_of_edges)]
-    near = exchange(volume, "near", lambda c: c)
-    near_halos = [exchange(halo, "near", lambda c: c) for halo in own_halos]
+    turns = [[], [lambda c: 1 - c]][chans - 1] if chans <= 2 else [lambda c: c + 1, lambda c: c - 1]
+    same = lambda c: c
+    near = exchange(volume, "near", same)
+    token = call(early, [], [((8, LANES), F32)], [], WEIGHT_COPY_FLOPS, 4)[0]
+    rest_rows = size_y - 2 * len(turns)
+    *edges, rest = call(
+        functools.partial(split_rows, chans=chans),
+        [volume, token],
+        [((2, 2, depth, channels), BF16)] * len(turns) + [((2, rest_rows, depth, channels), BF16)],
+        [],
+        WEIGHT_COPY_FLOPS,
+        4,
+    )
+    own_halos = [exchange(edge, "own", turn) for edge, turn in zip(edges, turns)]
+    far_edges = [exchange(edge, "far", same) for edge in edges]
+    far_rest = exchange(rest, "far", same)
+    near_halos = [exchange(halo, "near", same) for halo in own_halos]
+    far_halos = [exchange(edge, "own", turn) for edge, turn in zip(far_edges, turns)]
 
     rows = size_y + min(chans - 1, 2)
     flops_of_plane = 2 * size_y * depth * 9 * channels * channels
-    static = dict(chans=chans, halo_count=len(edges))
+    static = dict(chans=chans, halo_count=len(turns))
     partials = call(
         functools.partial(kernel_a, **static),
         [volume, *own_halos, near, *near_halos, first_weight, second_weight],
@@ -289,7 +305,7 @@
     )
     skipped, pooled = call(
         functools.partial(kernel_b, **static),
-        [far, *far_halos, *partials, first_weight, second_weight],
+        [far_rest, *far_edges, *far_halos, *partials, first_weight, second_weight],
         [(volume.shape, BF16), ((size_y // 2, depth // 2, channels), BF16)],
         [
             pltpu.VMEM((2, size_y + 4, depth, channels), BF16),
@@ -303,7 +319,7 @@
     turns = [(lambda c, step=step: (c + step) % chans) for step in range(chans)]
     own_blocks = [pooled] + [exchange(pooled, "own", turn) for turn in turns[1:]]
     far_blocks = [exchange(pooled, "far", turns[0])]
-    far_blocks += [exchange(pooled, "far", turn) for turn in turns[1:]]
+    far_blocks += [exchange(block, "far", turns[0]) for block in own_blocks[1:]]
     near_blocks = [exchange(pooled, "near", turns[0])]
     near_blocks += [exchange(block, "near", turns[0]) for block in own_blocks[1:]]
     part_shape = (size_y // 2, depth // 2, channels)

time: 49.8 us -> 42.7 us (0.86)
  the two profiles are of different devices: /device:TPU:1 before, /device:TPU:16 now
where the time goes in v1:
time: 42.7 us; the launch traced here: 42.5 us
  starting transfers between devices  17.3 us (41%)
  Pallas kernels  15 us (35%)
  waiting for transfers between devices  9.01 us (21%)
  local copies, waits for them, and re-layouts  1.05 us (2%)
    ppermute x12, starting transfers between devices, exchange(): return lax.ppermute(value, AXES, pairs)  17.3 us
    pallas_call x6, Pallas kernels, call(): pl.pallas_call(kernel, out_shape=out_shape, in_specs=[VMEM_SPEC] * len(in...  15 us
    ppermute x12, waiting for transfers between devices, exchange(): return lax.ppermute(value, AXES, pairs)  9.01 us
    unnamed x10, local copies, waits for them, and re-layouts  1.05 us
  transfers between devices with their start and end apart: 12, of which 4 were waited for; matrix products, arithmetic and copies ran while one was open for 0% of the time, Pallas kernels for 20%

profile of v1, /device:TPU:16, one launch (start us, length us, event | category | flops | bytes accessed | tf_op | source)
XLA Modules:
  0.0 42.5 jit_solution(9114193210733593058)
XLA Ops:
  0.0 0.0 collective-permute-start.4
  0.0 1.0 %copy-done.4 = bf16[2,8,64,256]{3,2,1,0:T(8,128)(2,1)S(1)} copy-done((bf16[2,8,64,256]{3,2,1,0:T(8,128)(2,1)S(1)}, bf16[2,8,64,256]{3,2,1,0:T(8,128)(2,1)}, u32[]{:S(2)}) %copy-start.4) | copy-done | bytes 524312
  1.1 1.6 %collective-permute-start.3 = (bf16[2,2,64,256]{3,2,1,0:T(8,128)(2,1)S(1)}, bf16[2,2,64,256]{3,2,1,0:T(8,128)(2,1)S(1)}, u32[]{:S(2)}, u32[]{:S(2)}) collective-permute-start(bf16[2,2,64,256]{3,2,1,0:T(8,128)(2,1)S(1)} %get-tuple-element.16), channel_id=1, source_target_pairs={{0,1},{1,0},{2,3},{3,2},{4,5},{5,4},{6,7},{7,6},{8,9},{9,8},{10,11... | collective-permute-start | bytes 393224 | tf_op jit(solution)/shard_map/ppermute | solution.py:34
  2.6 2.6 %collective-permute-start.1 = (bf16[2,2,64,256]{3,2,1,0:T(8,128)(2,1)S(1)}, bf16[2,2,64,256]{3,2,1,0:T(8,128)(2,1)S(1)}, u32[]{:S(2)}, u32[]{:S(2)}) collective-permute-start(bf16[2,2,64,256]{3,2,1,0:T(8,128)(2,1)S(1)} %get-tuple-element.16), channel_id=1, source_target_pairs={{2,4},{3,5},{4,2},{5,3},{6,8},{7,9},{8,6},{9,7},{10,12},{11,13},{1... | collective-permute-start | bytes 393224 | tf_op jit(solution)/shard_map/ppermute | solution.py:34
  5.2 1.1 %collective-permute-done.3.refs_1_ = bf16[2,2,64,256]{3,2,1,0:T(8,128)(2,1)S(1)} collective-permute-done((bf16[2,2,64,256]{3,2,1,0:T(8,128)(2,1)S(1)}, bf16[2,2,64,256]{3,2,1,0:T(8,128)(2,1)S(1)}, u32[]{:S(2)}, u32[]{:S(2)}) %collective-permute-start.3) | collective-permute-done | bytes 131104 | tf_op jit(solution)/shard_map/ppermute | solution.py:34
  6.4 0.0 collective-permute-start.5
  6.4 3.4 %collective-permute-start = (bf16[2,6,64,256]{3,2,1,0:T(8,128)(2,1)S(1)}, bf16[2,6,64,256]{3,2,1,0:T(8,128)(2,1)S(1)}, u32[]{:S(2)}, u32[]{:S(2)}) collective-permute-start(bf16[2,6,64,256]{3,2,1,0:T(8,128)(2,1)S(1)} %get-tuple-element.15), channel_id=1, source_target_pairs={{2,4},{3,5},{4,2},{5,3},{6,8},{7,9},{8,6},{9,7},{10,12},{11,13},{1... | collective-permute-start | bytes 1179656 | tf_op jit(solution)/shard_map/ppermute | solution.py:34
  9.8 0.2 collective-permute-done.1.refs_1_
  10.1 1.3 %collective-permute-start.2 = (bf16[2,2,64,256]{3,2,1,0:T(8,128)(2,1)S(1)}, bf16[2,2,64,256]{3,2,1,0:T(8,128)(2,1)S(1)}, u32[]{:S(2)}, u32[]{:S(2)}) collective-permute-start(bf16[2,2,64,256]{3,2,1,0:T(8,128)(2,1)S(1)} %collective-permute-done.1.refs_1_), channel_id=1, source_target_pairs={{0,1},{1,0},{2,3},{3,2},{4,5},{5,4},{6,7},{7,6},{8,9},{9,8},{10,11... | collective-permute-start | bytes 393224 | tf_op jit(solution)/shard_map/ppermute | solution.py:34
  11.4 0.0 collective-permute-done.5.refs_3_
  11.4 0.0 collective-permute-done.4.refs_2_
  11.4 0.0 copy-done.2
  11.4 8.4 %shard_map.57 = (f32[9,64,256]{2,1,0:T(8,128)S(1)}, f32[9,64,256]{2,1,0:T(8,128)S(1)}, f32[8,64,256]{2,1,0:T(8,128)S(1)}, f32[8,64,256]{2,1,0:T(8,128)S(1)}) custom-call(bf16[2,8,64,256]{3,2,1,0:T(8,128)(2,1)S(1)} %copy-done.4, bf16[2,2,64,256]{3,2,1,0:T(8,128)(2,1)S(1)} %collective-permute-done.3.refs_1_, ...), custom_call_target="tpu_custom_call" | custom-call | flops 7247757312 | bytes 1048576 | tf_op jit(solution)/shard_map/pallas_call | solution.py:62
  19.8 0.0 collective-permute-done.2.refs_2_
  19.8 0.0 collective-permute-done.refs_0_
  19.8 0.0 copy-start
  19.8 0.0 copy-start.1
  19.8 4.4 %shard_map.58 = (bf16[2,8,64,256]{3,2,1,0:T(8,128)(2,1)S(1)}, bf16[4,32,256]{2,1,0:T(8,128)(2,1)S(1)}) custom-call(bf16[2,6,64,256]{3,2,1,0:T(8,128)(2,1)S(1)} %collective-permute-done.refs_0_, bf16[2,2,64,256]{3,2,1,0:T(8,128)(2,1)S(1)} %collective-permute-done.1.refs_1_, bf16[2,2,64,256]{3,2,1,0:T(8,128)(2,1)S(1)} %collective-permute-done.2.refs_2_, ...), custom_call_target="tpu_custom_call" | custom-call | flops 3623878656 | bytes 1048576 | tf_op jit(solution)/shard_map/pallas_call | solution.py:62
  24.2 0.7 %collective-permute-start.7 = (bf16[4,32,256]{2,1,0:T(8,128)(2,1)S(1)}, bf16[4,32,256]{2,1,0:T(8,128)(2,1)S(1)}, u32[]{:S(2)}, u32[]{:S(2)}) collective-permute-start(bf16[4,32,256]{2,1,0:T(8,128)(2,1)S(1)} %get-tuple-element.22.refs_2_), channel_id=1, source_target_pairs={{0,1},{1,0},{2,3},{3,2},{4,5},{5,4},{6,7},{7,6},{8,9},{9,8},{10,11... | collective-permute-start | bytes 196616 | tf_op jit(solution)/shard_map/ppermute | solution.py:34
  25.0 2.3 %collective-permute-start.6 = (bf16[4,32,256]{2,1,0:T(8,128)(2,1)S(1)}, bf16[4,32,256]{2,1,0:T(8,128)(2,1)S(1)}, u32[]{:S(2)}, u32[]{:S(2)}) collective-permute-start(bf16[4,32,256]{2,1,0:T(8,128)(2,1)S(1)} %get-tuple-element.22.refs_2_), channel_id=1, source_target_pairs={{2,4},{3,5},{4,2},{5,3},{6,8},{7,9},{8,6},{9,7},{10,12},{11,13},{1... | collective-permute-start | bytes 196616 | tf_op jit(solution)/shard_map/ppermute | solution.py:34
  27.3 2.0 %collective-permute-start.9 = (bf16[4,32,256]{2,1,0:T(8,128)(2,1)S(1)}, bf16[4,32,256]{2,1,0:T(8,128)(2,1)S(1)}, u32[]{:S(2)}, u32[]{:S(2)}) collective-permute-start(bf16[4,32,256]{2,1,0:T(8,128)(2,1)S(1)} %get-tuple-element.22.refs_2_), channel_id=1, source_target_pairs={{0,2},{1,3},{2,0},{3,1},{4,6},{5,7},{6,4},{7,5},{8,10},{9,11},{10,... | collective-permute-start | bytes 196616 | tf_op jit(solution)/shard_map/ppermute | solution.py:34
  29.3 0.0 collective-permute-done.7.refs_3_
  29.3 0.1 collective-permute-start.10
  29.4 2.7 %collective-permute-start.8 = (bf16[4,32,256]{2,1,0:T(8,128)(2,1)S(1)}, bf16[4,32,256]{2,1,0:T(8,128)(2,1)S(1)}, u32[]{:S(2)}, u32[]{:S(2)}) collective-permute-start(bf16[4,32,256]{2,1,0:T(8,128)(2,1)S(1)} %collective-permute-done.7.refs_3_), channel_id=1, source_target_pairs={{2,4},{3,5},{4,2},{5,3},{6,8},{7,9},{8,6},{9,7},{10,12},{11,13},{1... | collective-permute-start | bytes 196616 | tf_op jit(solution)/shard_map/ppermute | solution.py:34
  32.0 0.0 collective-permute-done.6.refs_0_
  32.0 0.0 collective-permute-done.9.refs_4_
  32.0 0.0 collective-permute-done.10.refs_5_
  32.1 3.9 %collective-permute-done.8.refs_1_ = bf16[4,32,256]{2,1,0:T(8,128)(2,1)S(1)} collective-permute-done((bf16[4,32,256]{2,1,0:T(8,128)(2,1)S(1)}, bf16[4,32,256]{2,1,0:T(8,128)(2,1)S(1)}, u32[]{:S(2)}, u32[]{:S(2)}) %collective-permute-start.8) | collective-permute-done | bytes 65568 | tf_op jit(solution)/shard_map/ppermute | solution.py:34
  35.9 1.3 %shard_map.59 = (f32[4,32,256]{2,1,0:T(8,128)S(1)}, bf16[4,32,256]{2,1,0:T(8,128)(2,1)S(1)}) custom-call(bf16[4,32,256]{2,1,0:T(8,128)(2,1)S(1)} %collective-permute-done.6.refs_0_, bf16[4,32,256]{2,1,0:T(8,128)(2,1)S(1)} %collective-permute-done.8.refs_1_, bf16[4,32,256]{2,1,0:T(8,128)(2,1)S(1)} %get-tuple-element.22.refs_2_, ...), custom_call_target="tpu_custom_call" | custom-call | flops 905969664 | bytes 1048576 | tf_op jit(solution)/shard_map/pallas_call | solution.py:62
  37.2 0.6 %collective-permute-start.11 = (bf16[4,32,256]{2,1,0:T(8,128)(2,1)S(1)}, bf16[4,32,256]{2,1,0:T(8,128)(2,1)S(1)}, u32[]{:S(2)}, u32[]{:S(2)}) collective-permute-start(bf16[4,32,256]{2,1,0:T(8,128)(2,1)S(1)} %get-tuple-element.24), channel_id=1, source_target_pairs={{0,1},{1,0},{2,3},{3,2},{4,5},{5,4},{6,7},{7,6},{8,9},{9,8},{10,11... | collective-permute-start | bytes 196616 | tf_op jit(solution)/shard_map/ppermute | solution.py:34
  37.8 3.7 %collective-permute-done.11.refs_2_ = bf16[4,32,256]{2,1,0:T(8,128)(2,1)S(1)} collective-permute-done((bf16[4,32,256]{2,1,0:T(8,128)(2,1)S(1)}, bf16[4,32,256]{2,1,0:T(8,128)(2,1)S(1)}, u32[]{:S(2)}, u32[]{:S(2)}) %collective-permute-start.11) | collective-permute-done | bytes 65568 | tf_op jit(solution)/shard_map/ppermute | solution.py:34
  41.6 0.9 %shard_map.60 = bf16[2,8,64,256]{3,2,1,0:T(8,128)(2,1)} custom-call(bf16[2,8,64,256]{3,2,1,0:T(8,128)(2,1)S(1)} %get-tuple-element.21.refs_0_, f32[4,32,256]{2,1,0:T(8,128)S(1)} %get-tuple-element.23.refs_1_, bf16[4,32,256]{2,1,0:T(8,128)(2,1)S(1)} %collective-permute-done.11.refs_2_), custom_call_target="tpu_custom_call" | custom-call | flops 262144 | bytes 1048576 | tf_op jit(solution)/shard_map/pallas_call | solution.py:62
  (8 shorter events, 0.0 us)
Async XLA Ops:
  0.0 1.0 %copy-start.4 = (bf16[2,8,64,256]{3,2,1,0:T(8,128)(2,1)S(1)}, bf16[2,8,64,256]{3,2,1,0:T(8,128)(2,1)}, u32[]{:S(2)}) copy-start(bf16[2,8,64,256]{3,2,1,0:T(8,128)(2,1)} %refs_0_.1) | copy-start | bytes 1572868
  0.0 11.4 %collective-permute-start.4 = (bf16[2,8,64,256]{3,2,1,0:T(8,128)(2,1)}, bf16[2,8,64,256]{3,2,1,0:T(8,128)(2,1)S(1)}, u32[]{:S(2)}, u32[]{:S(2)}) collective-permute-start(bf16[2,8,64,256]{3,2,1,0:T(8,128)(2,1)} %refs_0_.1), channel_id=1, source_target_pairs={{0,2},{1,3},{2,0},{3,1},{4,6},{5,7},{6,4},{7,5},{8,10},{9,11},{10,... | collective-permute-start | bytes 1572872 | tf_op jit(solution)/shard_map/ppermute | solution.py:34
  1.0 10.3 %copy-start.2 = (bf16[3,3,3,256,256]{4,3,2,1,0:T(8,128)(2,1)S(1)}, bf16[3,3,3,256,256]{4,3,2,1,0:T(8,128)(2,1)}, u32[]{:S(2)}) copy-start(bf16[3,3,3,256,256]{4,3,2,1,0:T(8,128)(2,1)} %refs_7_.2) | copy-start | bytes 10616836
  1.0 10.3 %copy-start.3 = (bf16[3,3,3,256,256]{4,3,2,1,0:T(8,128)(2,1)S(1)}, bf16[3,3,3,256,256]{4,3,2,1,0:T(8,128)(2,1)}, u32[]{:S(2)}) copy-start(bf16[3,3,3,256,256]{4,3,2,1,0:T(8,128)(2,1)} %refs_8_.1) | copy-start | bytes 10616836
  1.1 5.3 %collective-permute-start.3 = (bf16[2,2,64,256]{3,2,1,0:T(8,128)(2,1)S(1)}, bf16[2,2,64,256]{3,2,1,0:T(8,128)(2,1)S(1)}, u32[]{:S(2)}, u32[]{:S(2)}) collective-permute-start(bf16[2,2,64,256]{3,2,1,0:T(8,128)(2,1)S(1)} %get-tuple-element.16), channel_id=1, source_target_pairs={{0,1},{1,0},{2,3},{3,2},{4,5},{5,4},{6,7},{7,6},{8,9},{9,8},{10,11... | collective-permute-start | bytes 393224 | tf_op jit(solution)/shard_map/ppermute | solution.py:34
  2.6 7.4 %collective-permute-start.1 = (bf16[2,2,64,256]{3,2,1,0:T(8,128)(2,1)S(1)}, bf16[2,2,64,256]{3,2,1,0:T(8,128)(2,1)S(1)}, u32[]{:S(2)}, u32[]{:S(2)}) collective-permute-start(bf16[2,2,64,256]{3,2,1,0:T(8,128)(2,1)S(1)} %get-tuple-element.16), channel_id=1, source_target_pairs={{2,4},{3,5},{4,2},{5,3},{6,8},{7,9},{8,6},{9,7},{10,12},{11,13},{1... | collective-permute-start | bytes 393224 | tf_op jit(solution)/shard_map/ppermute | solution.py:34
  6.4 5.0 %collective-permute-start.5 = (bf16[2,2,64,256]{3,2,1,0:T(8,128)(2,1)S(1)}, bf16[2,2,64,256]{3,2,1,0:T(8,128)(2,1)S(1)}, u32[]{:S(2)}, u32[]{:S(2)}) collective-permute-start(bf16[2,2,64,256]{3,2,1,0:T(8,128)(2,1)S(1)} %collective-permute-done.3.refs_1_), channel_id=1, source_target_pairs={{0,2},{1,3},{2,0},{3,1},{4,6},{5,7},{6,4},{7,5},{8,10},{9,11},{10,... | collective-permute-start | bytes 393224 | tf_op jit(solution)/shard_map/ppermute | solution.py:34
  6.4 13.4 %collective-permute-start = (bf16[2,6,64,256]{3,2,1,0:T(8,128)(2,1)S(1)}, bf16[2,6,64,256]{3,2,1,0:T(8,128)(2,1)S(1)}, u32[]{:S(2)}, u32[]{:S(2)}) collective-permute-start(bf16[2,6,64,256]{3,2,1,0:T(8,128)(2,1)S(1)} %get-tuple-element.15), channel_id=1, source_target_pairs={{2,4},{3,5},{4,2},{5,3},{6,8},{7,9},{8,6},{9,7},{10,12},{11,13},{1... | collective-permute-start | bytes 1179656 | tf_op jit(solution)/shard_map/ppermute | solution.py:34
  10.1 9.7 %collective-permute-start.2 = (bf16[2,2,64,256]{3,2,1,0:T(8,128)(2,1)S(1)}, bf16[2,2,64,256]{3,2,1,0:T(8,128)(2,1)S(1)}, u32[]{:S(2)}, u32[]{:S(2)}) collective-permute-start(bf16[2,2,64,256]{3,2,1,0:T(8,128)(2,1)S(1)} %collective-permute-done.1.refs_1_), channel_id=1, source_target_pairs={{0,1},{1,0},{2,3},{3,2},{4,5},{5,4},{6,7},{7,6},{8,9},{9,8},{10,11... | collective-permute-start | bytes 393224 | tf_op jit(solution)/shard_map/ppermute | solution.py:34
  19.8 16.2 %copy-start = (bf16[3,3,3,256,256]{4,3,2,1,0:T(8,128)(2,1)S(1)}, bf16[3,3,3,256,256]{4,3,2,1,0:T(8,128)(2,1)}, u32[]{:S(2)}) copy-start(bf16[3,3,3,256,256]{4,3,2,1,0:T(8,128)(2,1)} %refs_6_.1) | copy-start | bytes 10616836
  19.8 16.1 %copy-start.1 = (bf16[256,256]{1,0:T(8,128)(2,1)S(1)}, bf16[256,256]{1,0:T(8,128)(2,1)}, u32[]{:S(2)}) copy-start(bf16[256,256]{1,0:T(8,128)(2,1)} %refs_7_.3) | copy-start | bytes 393220
  24.2 5.0 %collective-permute-start.7 = (bf16[4,32,256]{2,1,0:T(8,128)(2,1)S(1)}, bf16[4,32,256]{2,1,0:T(8,128)(2,1)S(1)}, u32[]{:S(2)}, u32[]{:S(2)}) collective-permute-start(bf16[4,32,256]{2,1,0:T(8,128)(2,1)S(1)} %get-tuple-element.22.refs_2_), channel_id=1, source_target_pairs={{0,1},{1,0},{2,3},{3,2},{4,5},{5,4},{6,7},{7,6},{8,9},{9,8},{10,11... | collective-permute-start | bytes 196616 | tf_op jit(solution)/shard_map/ppermute | solution.py:34
  25.0 7.0 %collective-permute-start.6 = (bf16[4,32,256]{2,1,0:T(8,128)(2,1)S(1)}, bf16[4,32,256]{2,1,0:T(8,128)(2,1)S(1)}, u32[]{:S(2)}, u32[]{:S(2)}) collective-permute-start(bf16[4,32,256]{2,1,0:T(8,128)(2,1)S(1)} %get-tuple-element.22.refs_2_), channel_id=1, source_target_pairs={{2,4},{3,5},{4,2},{5,3},{6,8},{7,9},{8,6},{9,7},{10,12},{11,13},{1... | collective-permute-start | bytes 196616 | tf_op jit(solution)/shard_map/ppermute | solution.py:34
  27.3 4.7 %collective-permute-start.9 = (bf16[4,32,256]{2,1,0:T(8,128)(2,1)S(1)}, bf16[4,32,256]{2,1,0:T(8,128)(2,1)S(1)}, u32[]{:S(2)}, u32[]{:S(2)}) collective-permute-start(bf16[4,32,256]{2,1,0:T(8,128)(2,1)S(1)} %get-tuple-element.22.refs_2_), channel_id=1, source_target_pairs={{0,2},{1,3},{2,0},{3,1},{4,6},{5,7},{6,4},{7,5},{8,10},{9,11},{10,... | collective-permute-start | bytes 196616 | tf_op jit(solution)/shard_map/ppermute | solution.py:34
  29.3 2.8 %collective-permute-start.10 = (bf16[4,32,256]{2,1,0:T(8,128)(2,1)S(1)}, bf16[4,32,256]{2,1,0:T(8,128)(2,1)S(1)}, u32[]{:S(2)}, u32[]{:S(2)}) collective-permute-start(bf16[4,32,256]{2,1,0:T(8,128)(2,1)S(1)} %collective-permute-done.7.refs_3_), channel_id=1, source_target_pairs={{0,2},{1,3},{2,0},{3,1},{4,6},{5,7},{6,4},{7,5},{8,10},{9,11},{10,... | collective-permute-start | bytes 196616 | tf_op jit(solution)/shard_map/ppermute | solution.py:34
  29.4 6.6 %collective-permute-start.8 = (bf16[4,32,256]{2,1,0:T(8,128)(2,1)S(1)}, bf16[4,32,256]{2,1,0:T(8,128)(2,1)S(1)}, u32[]{:S(2)}, u32[]{:S(2)}) collective-permute-start(bf16[4,32,256]{2,1,0:T(8,128)(2,1)S(1)} %collective-permute-done.7.refs_3_), channel_id=1, source_target_pairs={{2,4},{3,5},{4,2},{5,3},{6,8},{7,9},{8,6},{9,7},{10,12},{11,13},{1... | collective-permute-start | bytes 196616 | tf_op jit(solution)/shard_map/ppermute | solution.py:34
  37.2 4.3 %collective-permute-start.11 = (bf16[4,32,256]{2,1,0:T(8,128)(2,1)S(1)}, bf16[4,32,256]{2,1,0:T(8,128)(2,1)S(1)}, u32[]{:S(2)}, u32[]{:S(2)}) collective-permute-start(bf16[4,32,256]{2,1,0:T(8,128)(2,1)S(1)} %get-tuple-element.24), channel_id=1, source_target_pairs={{0,1},{1,0},{2,3},{3,2},{4,5},{5,4},{6,7},{7,6},{8,9},{9,8},{10,11... | collective-permute-start | bytes 196616 | tf_op jit(solution)/shard_map/ppermute | solution.py:34

commit v2 on v1

--- a/solution.py
+++ b/solution.py
@@ -23,15 +23,24 @@
     return partner if 0 <= partner < bricks else None
 
 
-def exchange(value, kind, chan_of):
+def exchange(value, kind, chan_of=None):
     bricks, chans = lax.axis_size("brick"), lax.axis_size("chan")
     pairs = []
     for brick in range(bricks):
         for chan in range(chans):
-            other, target = brick_partner(kind, brick, bricks), chan_of(chan)
-            if other is not None and target is not None and 0 <= target < chans:
+            other = brick_partner(kind, brick, bricks)
+            target = chan if chan_of is None else chan_of(chan)
+            if other is None and chans % 2 == 0:
+                other, target = brick, chan ^ 1
+            if other is not None and 0 <= target < chans:
                 pairs.append((brick * chans + chan, other * chans + target))
     return lax.ppermute(value, AXES, pairs)
+
+
+def has_far():
+    brick = lax.axis_index("brick")
+    edge = brick + lax.rem(brick, 2)
+    return jnp.logical_and(edge > 0, edge < lax.axis_size("brick"))
 
 
 def row_split(chans, size_y):
@@ -106,16 +115,20 @@
     return [(0, None), (size_y + 2, None)]
 
 
-def fill_planes(target, slot, plane, pieces, halos, chans):
+def fill_planes(target, slot, plane, pieces, halos, chans, valid=None):
+    def rows_of(block):
+        rows = block[plane]
+        return rows if valid is None else jnp.where(valid, rows, jnp.zeros_like(rows))
+
     size_y = target.shape[1] - 4
     for start, block in pieces:
-        target[slot, pl.ds(start + 2, block.shape[1])] = block[plane]
+        target[slot, pl.ds(start + 2, block.shape[1])] = rows_of(block)
     zeros = jnp.zeros((2,) + target.shape[2:], target.dtype)
     if chans == 1:
         target[slot, 0:2] = zeros
         target[slot, size_y + 2 : size_y + 4] = zeros
     for (place, empty), halo in zip(halo_plan(chans, size_y), halos):
-        target[slot, pl.ds(place, 2)] = halo[plane]
+        target[slot, pl.ds(place, 2)] = rows_of(halo)
         if empty is not None:
             target[slot, pl.ds(empty, 2)] = zeros
 
@@ -178,14 +191,13 @@
     rest, edges, far_halos = refs[0], refs[1 : 1 + halo_count], refs[1 + halo_count : 1 + 2 * halo_count]
     layer_far, layer_own, out_far, out_near, weight_one, weight_two = refs[1 + 2 * halo_count : 7 + 2 * halo_count]
     skipped, pooled, field, layer, sums = refs[7 + 2 * halo_count :]
-    brick = lax.axis_index("brick")
-    odd = lax.rem(brick, 2)
+    odd = lax.rem(lax.axis_index("brick"), 2)
     size_y, depth = out_far.shape[0], out_far.shape[1]
     sides, between = row_split(chans, size_y)
     far = [(start, edge) for (start, _), edge in zip(sides, edges)] + [(between[0], rest)]
-    fill_planes(field, 0, odd, far, far_halos, chans)
-    fill_planes(field, 1, 1 - odd, far, far_halos, chans)
-    inside = jnp.logical_and(brick + odd > 0, brick + odd < lax.axis_size("brick"))
+    inside = has_far()
+    fill_planes(field, 0, odd, far, far_halos, chans, inside)
+    fill_planes(field, 1, 1 - odd, far, far_halos, chans, inside)
     start = first_row(chans)
     rows = layer_far.shape[0]
     lines = tile_of(rows)
@@ -229,13 +241,17 @@
     chan = lax.axis_index("chan")
     rows, depth = blocks[0].shape[0], blocks[0].shape[1]
     total = chans * rows
+    inside = has_far()
     for plane in range(3):
         zeros = jnp.zeros(field.shape[2:], field.dtype)
         field[plane, 0] = zeros
         field[plane, total + 1] = zeros
         for step in range(chans):
             source = lax.rem(chan - step + chans, chans)
-            field[plane, pl.ds(1 + source * rows, rows)] = blocks[plane * chans + step][...]
+            block = blocks[plane * chans + step][...]
+            if plane == 0:
+                block = jnp.where(inside, block, jnp.zeros_like(block))
+            field[plane, pl.ds(1 + source * rows, rows)] = block
     lines = tile_of(total)
     for row in range(0, total, lines):
         value = conv_lines([(field, step, tap(step, odd)) for step in range(3)], row, lines, weight)
@@ -274,8 +290,7 @@
     assert size_x == 2 and lax.axis_size("brick") % 2 == 0
 
     turns = [[], [lambda c: 1 - c]][chans - 1] if chans <= 2 else [lambda c: c + 1, lambda c: c - 1]
-    same = lambda c: c
-    near = exchange(volume, "near", same)
+    near = exchange(volume, "near")
     token = call(early, [], [((8, LANES), F32)], [], WEIGHT_COPY_FLOPS, 4)[0]
     rest_rows = size_y - 2 * len(turns)
     *edges, rest = call(
@@ -287,9 +302,9 @@
         4,
     )
     own_halos = [exchange(edge, "own", turn) for edge, turn in zip(edges, turns)]
-    far_edges = [exchange(edge, "far", same) for edge in edges]
-    far_rest = exchange(rest, "far", same)
-    near_halos = [exchange(halo, "near", same) for halo in own_halos]
+    far_edges = [exchange(edge, "far") for edge in edges]
+    far_rest = exchange(rest, "far")
+    near_halos = [exchange(halo, "near") for halo in own_halos]
     far_halos = [exchange(edge, "own", turn) for edge, turn in zip(far_edges, turns)]
 
     rows = size_y + min(chans - 1, 2)
@@ -318,10 +333,10 @@
 
     turns = [(lambda c, step=step: (c + step) % chans) for step in range(chans)]
     own_blocks = [pooled] + [exchange(pooled, "own", turn) for turn in turns[1:]]
-    far_blocks = [exchange(pooled, "far", turns[0])]
-    far_blocks += [exchange(block, "far", turns[0]) for block in own_blocks[1:]]
-    near_blocks = [exchange(pooled, "near", turns[0])]
-    near_blocks += [exchange(block, "near", turns[0]) for block in own_blocks[1:]]
+    far_blocks = [exchange(pooled, "far")]
+    far_blocks += [exchange(block, "far") for block in own_blocks[1:]]
+    near_blocks = [exchange(pooled, "near")]
+    near_blocks += [exchange(block, "near") for block in own_blocks[1:]]
     part_shape = (size_y // 2, depth // 2, channels)
     coarse_rows = chans * size_y // 2
     parts = call(

time: 42.7 us -> 38.9 us (0.911)
  the two profiles are of different devices: /device:TPU:16 before, /device:TPU:0 now
where the time goes in v2:
time: 38.9 us; the launch traced here: 38.8 us
  Pallas kernels  15 us (39%)
  starting transfers between devices  11.6 us (30%)
  waiting for transfers between devices  11.5 us (30%)
  local copies, waits for them, and re-layouts  0.57 us (1%)
    pallas_call x6, Pallas kernels, call(): pl.pallas_call(kernel, out_shape=out_shape, in_specs=[VMEM_SPEC] * len(in...  15 us
    ppermute x12, starting transfers between devices, exchange(): return lax.ppermute(value, AXES, pairs)  11.6 us
    ppermute x12, waiting for transfers between devices, exchange(): return lax.ppermute(value, AXES, pairs)  11.5 us
  transfers between devices with their start and end apart: 12, of which 5 were waited for; matrix products, arithmetic and copies ran while one was open for 0% of the time, Pallas kernels for 22%

profile of v2, /device:TPU:0, one launch (start us, length us, event | category | flops | bytes accessed | tf_op | source)
XLA Modules:
  0.0 38.8 jit_solution(12966110052358888309)
XLA Ops:
  0.0 0.5 %collective-permute-start.4 = (bf16[2,8,64,256]{3,2,1,0:T(8,128)(2,1)}, bf16[2,8,64,256]{3,2,1,0:T(8,128)(2,1)S(1)}, u32[]{:S(2)}, u32[]{:S(2)}) collective-permute-start(bf16[2,8,64,256]{3,2,1,0:T(8,128)(2,1)} %refs_0_.1), channel_id=1, source_target_pairs={{0,2},{1,3},{2,0},{3,1},{4,6},{5,7},{6,4},{7,5},{8,10},{9,11},{10,... | collective-permute-start | bytes 1572872 | tf_op jit(solution)/shard_map/ppermute | solution.py:37
  0.5 0.5 %copy-done.4 = bf16[2,8,64,256]{3,2,1,0:T(8,128)(2,1)S(1)} copy-done((bf16[2,8,64,256]{3,2,1,0:T(8,128)(2,1)S(1)}, bf16[2,8,64,256]{3,2,1,0:T(8,128)(2,1)}, u32[]{:S(2)}) %copy-start.4) | copy-done | bytes 524312
  1.1 3.0 %collective-permute-start.3 = (bf16[2,2,64,256]{3,2,1,0:T(8,128)(2,1)S(1)}, bf16[2,2,64,256]{3,2,1,0:T(8,128)(2,1)S(1)}, u32[]{:S(2)}, u32[]{:S(2)}) collective-permute-start(bf16[2,2,64,256]{3,2,1,0:T(8,128)(2,1)S(1)} %get-tuple-element.16), channel_id=1, source_target_pairs={{0,1},{1,0},{2,3},{3,2},{4,5},{5,4},{6,7},{7,6},{8,9},{9,8},{10,11... | collective-permute-start | bytes 393224 | tf_op jit(solution)/shard_map/ppermute | solution.py:37
  4.1 0.1 collective-permute-start.1
  4.2 3.4 %collective-permute-done.3.refs_1_ = bf16[2,2,64,256]{3,2,1,0:T(8,128)(2,1)S(1)} collective-permute-done((bf16[2,2,64,256]{3,2,1,0:T(8,128)(2,1)S(1)}, bf16[2,2,64,256]{3,2,1,0:T(8,128)(2,1)S(1)}, u32[]{:S(2)}, u32[]{:S(2)}) %collective-permute-start.3) | collective-permute-done | bytes 131104 | tf_op jit(solution)/shard_map/ppermute | solution.py:37
  7.6 0.0 collective-permute-start.5
  7.6 1.7 %collective-permute-start = (bf16[2,6,64,256]{3,2,1,0:T(8,128)(2,1)S(1)}, bf16[2,6,64,256]{3,2,1,0:T(8,128)(2,1)S(1)}, u32[]{:S(2)}, u32[]{:S(2)}) collective-permute-start(bf16[2,6,64,256]{3,2,1,0:T(8,128)(2,1)S(1)} %get-tuple-element.15), channel_id=1, source_target_pairs={{0,1},{1,0},{2,4},{3,5},{4,2},{5,3},{6,8},{7,9},{8,6},{9,7},{10,12... | collective-permute-start | bytes 1179656 | tf_op jit(solution)/shard_map/ppermute | solution.py:37
  9.4 0.0 collective-permute-done.1.refs_1_
  9.4 1.4 %collective-permute-start.2 = (bf16[2,2,64,256]{3,2,1,0:T(8,128)(2,1)S(1)}, bf16[2,2,64,256]{3,2,1,0:T(8,128)(2,1)S(1)}, u32[]{:S(2)}, u32[]{:S(2)}) collective-permute-start(bf16[2,2,64,256]{3,2,1,0:T(8,128)(2,1)S(1)} %collective-permute-done.1.refs_1_), channel_id=1, source_target_pairs={{0,1},{1,0},{2,3},{3,2},{4,5},{5,4},{6,7},{7,6},{8,9},{9,8},{10,11... | collective-permute-start | bytes 393224 | tf_op jit(solution)/shard_map/ppermute | solution.py:37
  10.8 0.0 collective-permute-done.5.refs_3_
  10.8 0.0 collective-permute-done.4.refs_2_
  10.8 0.0 copy-done.2
  10.8 8.4 %shard_map.57 = (f32[9,64,256]{2,1,0:T(8,128)S(1)}, f32[9,64,256]{2,1,0:T(8,128)S(1)}, f32[8,64,256]{2,1,0:T(8,128)S(1)}, f32[8,64,256]{2,1,0:T(8,128)S(1)}) custom-call(bf16[2,8,64,256]{3,2,1,0:T(8,128)(2,1)S(1)} %copy-done.4, bf16[2,2,64,256]{3,2,1,0:T(8,128)(2,1)S(1)} %collective-permute-done.3.refs_1_, ...), custom_call_target="tpu_custom_call" | custom-call | flops 7247757312 | bytes 1048576 | tf_op jit(solution)/shard_map/pallas_call | solution.py:71
  19.1 0.0 collective-permute-done.2.refs_2_
  19.2 0.0 collective-permute-done.refs_0_
  19.2 0.0 copy-start
  19.2 0.0 copy-start.1
  19.2 4.4 %shard_map.58 = (bf16[2,8,64,256]{3,2,1,0:T(8,128)(2,1)S(1)}, bf16[4,32,256]{2,1,0:T(8,128)(2,1)S(1)}) custom-call(bf16[2,6,64,256]{3,2,1,0:T(8,128)(2,1)S(1)} %collective-permute-done.refs_0_, bf16[2,2,64,256]{3,2,1,0:T(8,128)(2,1)S(1)} %collective-permute-done.1.refs_1_, bf16[2,2,64,256]{3,2,1,0:T(8,128)(2,1)S(1)} %collective-permute-done.2.refs_2_, ...), custom_call_target="tpu_custom_call" | custom-call | flops 3623878656 | bytes 1048576 | tf_op jit(solution)/shard_map/pallas_call | solution.py:71
  23.6 0.8 %collective-permute-start.7 = (bf16[4,32,256]{2,1,0:T(8,128)(2,1)S(1)}, bf16[4,32,256]{2,1,0:T(8,128)(2,1)S(1)}, u32[]{:S(2)}, u32[]{:S(2)}) collective-permute-start(bf16[4,32,256]{2,1,0:T(8,128)(2,1)S(1)} %get-tuple-element.22.refs_2_), channel_id=1, source_target_pairs={{0,1},{1,0},{2,3},{3,2},{4,5},{5,4},{6,7},{7,6},{8,9},{9,8},{10,11... | collective-permute-start | bytes 196616 | tf_op jit(solution)/shard_map/ppermute | solution.py:37
  24.5 1.3 %collective-permute-start.6 = (bf16[4,32,256]{2,1,0:T(8,128)(2,1)S(1)}, bf16[4,32,256]{2,1,0:T(8,128)(2,1)S(1)}, u32[]{:S(2)}, u32[]{:S(2)}) collective-permute-start(bf16[4,32,256]{2,1,0:T(8,128)(2,1)S(1)} %get-tuple-element.22.refs_2_), channel_id=1, source_target_pairs={{0,1},{1,0},{2,4},{3,5},{4,2},{5,3},{6,8},{7,9},{8,6},{9,7},{10,12... | collective-permute-start | bytes 196616 | tf_op jit(solution)/shard_map/ppermute | solution.py:37
  25.7 1.2 %collective-permute-start.9 = (bf16[4,32,256]{2,1,0:T(8,128)(2,1)S(1)}, bf16[4,32,256]{2,1,0:T(8,128)(2,1)S(1)}, u32[]{:S(2)}, u32[]{:S(2)}) collective-permute-start(bf16[4,32,256]{2,1,0:T(8,128)(2,1)S(1)} %get-tuple-element.22.refs_2_), channel_id=1, source_target_pairs={{0,2},{1,3},{2,0},{3,1},{4,6},{5,7},{6,4},{7,5},{8,10},{9,11},{10,... | collective-permute-start | bytes 196616 | tf_op jit(solution)/shard_map/ppermute | solution.py:37
  26.9 1.1 %collective-permute-done.7.refs_3_ = bf16[4,32,256]{2,1,0:T(8,128)(2,1)S(1)} collective-permute-done((bf16[4,32,256]{2,1,0:T(8,128)(2,1)S(1)}, bf16[4,32,256]{2,1,0:T(8,128)(2,1)S(1)}, u32[]{:S(2)}, u32[]{:S(2)}) %collective-permute-start.7) | collective-permute-done | bytes 65568 | tf_op jit(solution)/shard_map/ppermute | solution.py:37
  28.0 0.0 collective-permute-start.10
  28.0 0.8 %collective-permute-start.8 = (bf16[4,32,256]{2,1,0:T(8,128)(2,1)S(1)}, bf16[4,32,256]{2,1,0:T(8,128)(2,1)S(1)}, u32[]{:S(2)}, u32[]{:S(2)}) collective-permute-start(bf16[4,32,256]{2,1,0:T(8,128)(2,1)S(1)} %collective-permute-done.7.refs_3_), channel_id=1, source_target_pairs={{0,1},{1,0},{2,4},{3,5},{4,2},{5,3},{6,8},{7,9},{8,6},{9,7},{10,12... | collective-permute-start | bytes 196616 | tf_op jit(solution)/shard_map/ppermute | solution.py:37
  28.7 0.0 collective-permute-done.6.refs_0_
  28.7 0.0 collective-permute-done.9.refs_4_
  28.7 0.5 %collective-permute-done.10.refs_5_ = bf16[4,32,256]{2,1,0:T(8,128)(2,1)S(1)} collective-permute-done((bf16[4,32,256]{2,1,0:T(8,128)(2,1)S(1)}, bf16[4,32,256]{2,1,0:T(8,128)(2,1)S(1)}, u32[]{:S(2)}, u32[]{:S(2)}) %collective-permute-start.10) | collective-permute-done | bytes 65568 | tf_op jit(solution)/shard_map/ppermute | solution.py:37
  29.2 3.0 %collective-permute-done.8.refs_1_ = bf16[4,32,256]{2,1,0:T(8,128)(2,1)S(1)} collective-permute-done((bf16[4,32,256]{2,1,0:T(8,128)(2,1)S(1)}, bf16[4,32,256]{2,1,0:T(8,128)(2,1)S(1)}, u32[]{:S(2)}, u32[]{:S(2)}) %collective-permute-start.8) | collective-permute-done | bytes 65568 | tf_op jit(solution)/shard_map/ppermute | solution.py:37
  32.2 1.3 %shard_map.59 = (f32[4,32,256]{2,1,0:T(8,128)S(1)}, bf16[4,32,256]{2,1,0:T(8,128)(2,1)S(1)}) custom-call(bf16[4,32,256]{2,1,0:T(8,128)(2,1)S(1)} %collective-permute-done.6.refs_0_, bf16[4,32,256]{2,1,0:T(8,128)(2,1)S(1)} %collective-permute-done.8.refs_1_, bf16[4,32,256]{2,1,0:T(8,128)(2,1)S(1)} %get-tuple-element.22.refs_2_, ...), custom_call_target="tpu_custom_call" | custom-call | flops 905969664 | bytes 1048576 | tf_op jit(solution)/shard_map/pallas_call | solution.py:71
  33.5 0.8 %collective-permute-start.11 = (bf16[4,32,256]{2,1,0:T(8,128)(2,1)S(1)}, bf16[4,32,256]{2,1,0:T(8,128)(2,1)S(1)}, u32[]{:S(2)}, u32[]{:S(2)}) collective-permute-start(bf16[4,32,256]{2,1,0:T(8,128)(2,1)S(1)} %get-tuple-element.24), channel_id=1, source_target_pairs={{0,1},{1,0},{2,3},{3,2},{4,5},{5,4},{6,7},{7,6},{8,9},{9,8},{10,11... | collective-permute-start | bytes 196616 | tf_op jit(solution)/shard_map/ppermute | solution.py:37
  34.4 3.5 %collective-permute-done.11.refs_2_ = bf16[4,32,256]{2,1,0:T(8,128)(2,1)S(1)} collective-permute-done((bf16[4,32,256]{2,1,0:T(8,128)(2,1)S(1)}, bf16[4,32,256]{2,1,0:T(8,128)(2,1)S(1)}, u32[]{:S(2)}, u32[]{:S(2)}) %collective-permute-start.11) | collective-permute-done | bytes 65568 | tf_op jit(solution)/shard_map/ppermute | solution.py:37
  37.9 0.9 %shard_map.60 = bf16[2,8,64,256]{3,2,1,0:T(8,128)(2,1)} custom-call(bf16[2,8,64,256]{3,2,1,0:T(8,128)(2,1)S(1)} %get-tuple-element.21.refs_0_, f32[4,32,256]{2,1,0:T(8,128)S(1)} %get-tuple-element.23.refs_1_, bf16[4,32,256]{2,1,0:T(8,128)(2,1)S(1)} %collective-permute-done.11.refs_2_), custom_call_target="tpu_custom_call" | custom-call | flops 262144 | bytes 1048576 | tf_op jit(solution)/shard_map/pallas_call | solution.py:71
  (8 shorter events, 0.0 us)
Async XLA Ops:
  0.0 1.0 %copy-start.4 = (bf16[2,8,64,256]{3,2,1,0:T(8,128)(2,1)S(1)}, bf16[2,8,64,256]{3,2,1,0:T(8,128)(2,1)}, u32[]{:S(2)}) copy-start(bf16[2,8,64,256]{3,2,1,0:T(8,128)(2,1)} %refs_0_.1) | copy-start | bytes 1572868
  0.0 10.8 %collective-permute-start.4 = (bf16[2,8,64,256]{3,2,1,0:T(8,128)(2,1)}, bf16[2,8,64,256]{3,2,1,0:T(8,128)(2,1)S(1)}, u32[]{:S(2)}, u32[]{:S(2)}) collective-permute-start(bf16[2,8,64,256]{3,2,1,0:T(8,128)(2,1)} %refs_0_.1), channel_id=1, source_target_pairs={{0,2},{1,3},{2,0},{3,1},{4,6},{5,7},{6,4},{7,5},{8,10},{9,11},{10,... | collective-permute-start | bytes 1572872 | tf_op jit(solution)/shard_map/ppermute | solution.py:37
  1.0 9.7 %copy-start.2 = (bf16[3,3,3,256,256]{4,3,2,1,0:T(8,128)(2,1)S(1)}, bf16[3,3,3,256,256]{4,3,2,1,0:T(8,128)(2,1)}, u32[]{:S(2)}) copy-start(bf16[3,3,3,256,256]{4,3,2,1,0:T(8,128)(2,1)} %refs_7_.2) | copy-start | bytes 10616836
  1.0 9.7 %copy-start.3 = (bf16[3,3,3,256,256]{4,3,2,1,0:T(8,128)(2,1)S(1)}, bf16[3,3,3,256,256]{4,3,2,1,0:T(8,128)(2,1)}, u32[]{:S(2)}) copy-start(bf16[3,3,3,256,256]{4,3,2,1,0:T(8,128)(2,1)} %refs_8_.1) | copy-start | bytes 10616836
  1.1 6.5 %collective-permute-start.3 = (bf16[2,2,64,256]{3,2,1,0:T(8,128)(2,1)S(1)}, bf16[2,2,64,256]{3,2,1,0:T(8,128)(2,1)S(1)}, u32[]{:S(2)}, u32[]{:S(2)}) collective-permute-start(bf16[2,2,64,256]{3,2,1,0:T(8,128)(2,1)S(1)} %get-tuple-element.16), channel_id=1, source_target_pairs={{0,1},{1,0},{2,3},{3,2},{4,5},{5,4},{6,7},{7,6},{8,9},{9,8},{10,11... | collective-permute-start | bytes 393224 | tf_op jit(solution)/shard_map/ppermute | solution.py:37
  4.1 5.2 %collective-permute-start.1 = (bf16[2,2,64,256]{3,2,1,0:T(8,128)(2,1)S(1)}, bf16[2,2,64,256]{3,2,1,0:T(8,128)(2,1)S(1)}, u32[]{:S(2)}, u32[]{:S(2)}) collective-permute-start(bf16[2,2,64,256]{3,2,1,0:T(8,128)(2,1)S(1)} %get-tuple-element.16), channel_id=1, source_target_pairs={{0,1},{1,0},{2,4},{3,5},{4,2},{5,3},{6,8},{7,9},{8,6},{9,7},{10,12... | collective-permute-start | bytes 393224 | tf_op jit(solution)/shard_map/ppermute | solution.py:37
  7.6 3.1 %collective-permute-start.5 = (bf16[2,2,64,256]{3,2,1,0:T(8,128)(2,1)S(1)}, bf16[2,2,64,256]{3,2,1,0:T(8,128)(2,1)S(1)}, u32[]{:S(2)}, u32[]{:S(2)}) collective-permute-start(bf16[2,2,64,256]{3,2,1,0:T(8,128)(2,1)S(1)} %collective-permute-done.3.refs_1_), channel_id=1, source_target_pairs={{0,2},{1,3},{2,0},{3,1},{4,6},{5,7},{6,4},{7,5},{8,10},{9,11},{10,... | collective-permute-start | bytes 393224 | tf_op jit(solution)/shard_map/ppermute | solution.py:37
  7.6 11.5 %collective-permute-start = (bf16[2,6,64,256]{3,2,1,0:T(8,128)(2,1)S(1)}, bf16[2,6,64,256]{3,2,1,0:T(8,128)(2,1)S(1)}, u32[]{:S(2)}, u32[]{:S(2)}) collective-permute-start(bf16[2,6,64,256]{3,2,1,0:T(8,128)(2,1)S(1)} %get-tuple-element.15), channel_id=1, source_target_pairs={{0,1},{1,0},{2,4},{3,5},{4,2},{5,3},{6,8},{7,9},{8,6},{9,7},{10,12... | collective-permute-start | bytes 1179656 | tf_op jit(solution)/shard_map/ppermute | solution.py:37
  9.4 9.8 %collective-permute-start.2 = (bf16[2,2,64,256]{3,2,1,0:T(8,128)(2,1)S(1)}, bf16[2,2,64,256]{3,2,1,0:T(8,128)(2,1)S(1)}, u32[]{:S(2)}, u32[]{:S(2)}) collective-permute-start(bf16[2,2,64,256]{3,2,1,0:T(8,128)(2,1)S(1)} %collective-permute-done.1.refs_1_), channel_id=1, source_target_pairs={{0,1},{1,0},{2,3},{3,2},{4,5},{5,4},{6,7},{7,6},{8,9},{9,8},{10,11... | collective-permute-start | bytes 393224 | tf_op jit(solution)/shard_map/ppermute | solution.py:37
  19.2 13.1 %copy-start = (bf16[3,3,3,256,256]{4,3,2,1,0:T(8,128)(2,1)S(1)}, bf16[3,3,3,256,256]{4,3,2,1,0:T(8,128)(2,1)}, u32[]{:S(2)}) copy-start(bf16[3,3,3,256,256]{4,3,2,1,0:T(8,128)(2,1)} %refs_6_.1) | copy-start | bytes 10616836
  19.2 13.1 %copy-start.1 = (bf16[256,256]{1,0:T(8,128)(2,1)S(1)}, bf16[256,256]{1,0:T(8,128)(2,1)}, u32[]{:S(2)}) copy-start(bf16[256,256]{1,0:T(8,128)(2,1)} %refs_7_.3) | copy-start | bytes 393220
  23.6 4.3 %collective-permute-start.7 = (bf16[4,32,256]{2,1,0:T(8,128)(2,1)S(1)}, bf16[4,32,256]{2,1,0:T(8,128)(2,1)S(1)}, u32[]{:S(2)}, u32[]{:S(2)}) collective-permute-start(bf16[4,32,256]{2,1,0:T(8,128)(2,1)S(1)} %get-tuple-element.22.refs_2_), channel_id=1, source_target_pairs={{0,1},{1,0},{2,3},{3,2},{4,5},{5,4},{6,7},{7,6},{8,9},{9,8},{10,11... | collective-permute-start | bytes 196616 | tf_op jit(solution)/shard_map/ppermute | solution.py:37
  24.5 4.3 %collective-permute-start.6 = (bf16[4,32,256]{2,1,0:T(8,128)(2,1)S(1)}, bf16[4,32,256]{2,1,0:T(8,128)(2,1)S(1)}, u32[]{:S(2)}, u32[]{:S(2)}) collective-permute-start(bf16[4,32,256]{2,1,0:T(8,128)(2,1)S(1)} %get-tuple-element.22.refs_2_), channel_id=1, source_target_pairs={{0,1},{1,0},{2,4},{3,5},{4,2},{5,3},{6,8},{7,9},{8,6},{9,7},{10,12... | collective-permute-start | bytes 196616 | tf_op jit(solution)/shard_map/ppermute | solution.py:37
  25.7 3.0 %collective-permute-start.9 = (bf16[4,32,256]{2,1,0:T(8,128)(2,1)S(1)}, bf16[4,32,256]{2,1,0:T(8,128)(2,1)S(1)}, u32[]{:S(2)}, u32[]{:S(2)}) collective-permute-start(bf16[4,32,256]{2,1,0:T(8,128)(2,1)S(1)} %get-tuple-element.22.refs_2_), channel_id=1, source_target_pairs={{0,2},{1,3},{2,0},{3,1},{4,6},{5,7},{6,4},{7,5},{8,10},{9,11},{10,... | collective-permute-start | bytes 196616 | tf_op jit(solution)/shard_map/ppermute | solution.py:37
  28.0 1.3 %collective-permute-start.10 = (bf16[4,32,256]{2,1,0:T(8,128)(2,1)S(1)}, bf16[4,32,256]{2,1,0:T(8,128)(2,1)S(1)}, u32[]{:S(2)}, u32[]{:S(2)}) collective-permute-start(bf16[4,32,256]{2,1,0:T(8,128)(2,1)S(1)} %collective-permute-done.7.refs_3_), channel_id=1, source_target_pairs={{0,2},{1,3},{2,0},{3,1},{4,6},{5,7},{6,4},{7,5},{8,10},{9,11},{10,... | collective-permute-start | bytes 196616 | tf_op jit(solution)/shard_map/ppermute | solution.py:37
  28.0 4.3 %collective-permute-start.8 = (bf16[4,32,256]{2,1,0:T(8,128)(2,1)S(1)}, bf16[4,32,256]{2,1,0:T(8,128)(2,1)S(1)}, u32[]{:S(2)}, u32[]{:S(2)}) collective-permute-start(bf16[4,32,256]{2,1,0:T(8,128)(2,1)S(1)} %collective-permute-done.7.refs_3_), channel_id=1, source_target_pairs={{0,1},{1,0},{2,4},{3,5},{4,2},{5,3},{6,8},{7,9},{8,6},{9,7},{10,12... | collective-permute-start | bytes 196616 | tf_op jit(solution)/shard_map/ppermute | solution.py:37
  33.5 4.3 %collective-permute-start.11 = (bf16[4,32,256]{2,1,0:T(8,128)(2,1)S(1)}, bf16[4,32,256]{2,1,0:T(8,128)(2,1)S(1)}, u32[]{:S(2)}, u32[]{:S(2)}) collective-permute-start(bf16[4,32,256]{2,1,0:T(8,128)(2,1)S(1)} %get-tuple-element.24), channel_id=1, source_target_pairs={{0,1},{1,0},{2,3},{3,2},{4,5},{5,4},{6,7},{7,6},{8,9},{9,8},{10,11... | collective-permute-start | bytes 196616 | tf_op jit(solution)/shard_map/ppermute | solution.py:37
